TPU v7x, 128 devices: a whole 4x4x4 slice. The times are simulated.
128 devices in a mesh: pts: 64 (over z, x, y), grp: 2 (over core).
Axes of the slice: x: 4, y: 4, z: 4, core: 2. Of those that a mesh axis runs over, the one named last changes fastest.
Arguments:
- cam_jac: float32 [18, 1048576], P(None, ('pts', 'grp')), may hold values from -0.25 to 0.25
- pt_jac: float32 [6, 1048576], P(None, ('pts', 'grp')), may hold values from -6 to 6
- resid: float32 [2, 1048576], P(None, ('pts', 'grp')), may hold values from -102 to 102
- obs_point: int32 [1048576], P(('pts', 'grp')), may hold values from 0 to 262143, as said below
- obs_camera: int32 [1048576], P(('pts', 'grp')), may hold values from 0 to 2047
- camera_slot: int32 [2048], replicated, may hold values from 0 to 2047, each once
Outputs:
- cam_inverse: float32 [81, 2048], P(None, ('pts', 'grp'))
- precond: float32 [9, 1048576], P(None, ('pts', 'grp'))
Inputs may be any that keep to these rules, and one draw needn't show every extreme that they name: `obs_point`: observation o names a point of block o // 8192, from (o // 8192) * 2048 to (o // 8192 + 1) * 2048 - 1; within each block of 8192 observations the point number never falls and rises by at most 1 from one observation to the next, and the block's first observation names the block's first point. Each slot appears once; camera c is owned by device camera_slot[c] // 16 of the joined axes pts+grp.
All inputs are finite; a program needn't handle non-finite values.
Results may differ from a plain program's by a relative error of at most 0.0003.
Values sent between devices are 32-bit elements; how exact they have to be, the bound alone decides.
A program may use at most 64 MiB of HBM per device.

v0:
```python
import jax
import jax.numpy as jnp
from jax import lax
from jax.sharding import PartitionSpec as P

PTS_DEV = 2048
DAMP = 1.0
SPAN = 512


def split_up(value, dim, length):
    lengths = value.shape
    parts = value.reshape(*lengths[:dim], length, lengths[dim] // length, *lengths[dim + 1 :])
    return jnp.moveaxis(parts, dim, 0)


def sum_at_owner(value, axis, dim):
    length = lax.axis_size(axis)
    parts = lax.all_to_all(split_up(value, dim, length), axis, 0, 0, tiled=True)
    return jnp.sum(parts, axis=0)


def lower_pairs():
    return [(row_at, col_at) for row_at in range(9) for col_at in range(row_at + 1)]


def exact_dot(left, right):
    return jnp.dot(left, right, precision=lax.Precision.HIGHEST, preferred_element_type=jnp.float32)


def point_table(pt_jac, resid, local_point, npoints):
    entries = []
    for row_at in range(3):
        for col_at in range(row_at, 3):
            entries.append(
                pt_jac[row_at] * pt_jac[col_at] + pt_jac[3 + row_at] * pt_jac[3 + col_at]
            )
    for row_at in range(3):
        entries.append(pt_jac[row_at] * resid[0] + pt_jac[3 + row_at] * resid[1])
    stacked = jnp.stack(entries, 0)
    count = stacked.shape[1] // SPAN
    pieces = jnp.moveaxis(stacked.reshape(9, count, SPAN), 1, 0)
    point_rows = local_point.reshape(count, SPAN)
    firsts = point_rows[:, 0]
    window_ids = jnp.arange(SPAN, dtype=jnp.int32)

    def add_block(carry, inputs):
        piece, points, first = inputs
        onehot = (points[:, None] - first == window_ids[None, :]).astype(jnp.float32)
        window = lax.dynamic_slice_in_dim(carry, first, SPAN, 1)
        carry = lax.dynamic_update_slice_in_dim(carry, window + exact_dot(piece, onehot), first, 1)
        return (carry, None)

    sums, unused = lax.scan(
        add_block, jnp.zeros((9, npoints + SPAN), jnp.float32), (pieces, point_rows, firsts)
    )
    v00 = sums[0] + DAMP
    v01 = sums[1]
    v02 = sums[2]
    v11 = sums[3] + DAMP
    v12 = sums[4]
    v22 = sums[5] + DAMP
    c00 = v11 * v22 - v12 * v12
    c01 = v02 * v12 - v01 * v22
    c02 = v01 * v12 - v02 * v11
    c11 = v00 * v22 - v02 * v02
    c12 = v01 * v02 - v00 * v12
    c22 = v00 * v11 - v01 * v01
    determ = v00 * c00 + v01 * c01 + v02 * c02
    i00 = c00 / determ
    i01 = c01 / determ
    i02 = c02 / determ
    i11 = c11 / determ
    i12 = c12 / determ
    i22 = c22 / determ
    w_zero = i00 * sums[6] + i01 * sums[7] + i02 * sums[8]
    w_one = i01 * sums[6] + i11 * sums[7] + i12 * sums[8]
    w_two = i02 * sums[6] + i12 * sums[7] + i22 * sums[8]
    table = jnp.stack([i00, i01, i02, i11, i12, i22, w_zero, w_one, w_two], 0)

    def pick_block(carry, inputs):
        points, first = inputs
        onehot = (points[:, None] - first == window_ids[None, :]).astype(jnp.float32)
        window = lax.dynamic_slice_in_dim(table, first, SPAN, 1)
        return (carry, exact_dot(window, onehot.T))

    unused, picked = lax.scan(pick_block, 0, (point_rows, firsts))
    return jnp.moveaxis(picked, 0, 1).reshape(9, count * SPAN)


def obs_terms(cam_jac, pt_jac, resid, point_rows, pairs):
    i00, i01, i02, i11, i12, i22 = [point_rows[pos] for pos in range(6)]
    weights = [point_rows[6], point_rows[7], point_rows[8]]
    vinv = ((i00, i01, i02), (i01, i11, i12), (i02, i12, i22))
    prow = [[pt_jac[3 * rowp + inner] for inner in range(3)] for rowp in range(2)]
    usage = [
        [
            vinv[outer][0] * prow[rowp][0]
            + vinv[outer][1] * prow[rowp][1]
            + vinv[outer][2] * prow[rowp][2]
            for outer in range(3)
        ]
        for rowp in range(2)
    ]
    proj_zz = prow[0][0] * usage[0][0] + prow[0][1] * usage[0][1] + prow[0][2] * usage[0][2]
    proj_zo = prow[0][0] * usage[1][0] + prow[0][1] * usage[1][1] + prow[0][2] * usage[1][2]
    proj_oo = prow[1][0] * usage[1][0] + prow[1][1] * usage[1][1] + prow[1][2] * usage[1][2]
    keep = ((1.0 - proj_zz, -proj_zo), (-proj_zo, 1.0 - proj_oo))
    shifted = [
        resid[rowp]
        - (prow[rowp][0] * weights[0] + prow[rowp][1] * weights[1] + prow[rowp][2] * weights[2])
        for rowp in range(2)
    ]
    reduced = jnp.stack(
        [cam_jac[col_at] * shifted[0] + cam_jac[9 + col_at] * shifted[1] for col_at in range(9)], 0
    )
    mixed = [
        [
            keep[rowp][0] * cam_jac[col_at] + keep[rowp][1] * cam_jac[9 + col_at]
            for col_at in range(9)
        ]
        for rowp in range(2)
    ]
    terms = jnp.stack(
        [
            cam_jac[row_at] * mixed[0][col_at] + cam_jac[9 + row_at] * mixed[1][col_at]
            for row_at, col_at in pairs
        ],
        0,
    )
    return (terms, reduced)


def chol_inverse(rows, pairs):
    entry = {pair: rows[pos] for pos, pair in enumerate(pairs)}
    factor = {}
    for col_at in range(9):
        diag = entry[col_at, col_at] + DAMP
        for inner in range(col_at):
            diag = diag - factor[col_at, inner] * factor[col_at, inner]
        root = jnp.sqrt(diag)
        factor[col_at, col_at] = root
        for row_at in range(col_at + 1, 9):
            value = entry[row_at, col_at]
            for inner in range(col_at):
                value = value - factor[row_at, inner] * factor[col_at, inner]
            factor[row_at, col_at] = value / root
    solved = {}
    for col_at in range(9):
        solved[col_at, col_at] = 1.0 / factor[col_at, col_at]
        for row_at in range(col_at + 1, 9):
            value = factor[row_at, col_at] * solved[col_at, col_at]
            for inner in range(col_at + 1, row_at):
                value = value + factor[row_at, inner] * solved[inner, col_at]
            solved[row_at, col_at] = -value / factor[row_at, row_at]
    result = {}
    for row_at in range(9):
        for col_at in range(row_at + 1):
            value = solved[row_at, row_at] * solved[row_at, col_at]
            for inner in range(row_at + 1, 9):
                value = value + solved[inner, row_at] * solved[inner, col_at]
            result[row_at, col_at] = value
            result[col_at, row_at] = value
    return jnp.stack([result[row_at, col_at] for row_at in range(9) for col_at in range(9)], 0)


def apply_inverse(picked, reduced, locate):
    outputs = []
    for row_at in range(9):
        value = picked[locate[row_at, 0]] * reduced[0]
        for col_at in range(1, 9):
            value = value + picked[locate[row_at, col_at]] * reduced[col_at]
        outputs.append(value)
    return jnp.stack(outputs, 0)


def shards(cam_jac, pt_jac, resid, obs_point, obs_camera, camera_slot):
    cameras = camera_slot.shape[0]
    owned_count = cameras // lax.axis_size(("pts", "grp"))
    local_point = obs_point - lax.axis_index(("pts", "grp")) * PTS_DEV
    rows = point_table(pt_jac, resid, local_point, PTS_DEV)
    pairs = lower_pairs()
    terms, reduced = obs_terms(cam_jac, pt_jac, resid, rows, pairs)
    width = len(pairs)
    camera_of_slot = (
        jnp.zeros((cameras,), jnp.int32).at[camera_slot].set(jnp.arange(cameras, dtype=jnp.int32))
    )
    count = terms.shape[1] // SPAN
    term_blocks = jnp.moveaxis(terms.reshape(width, count, SPAN), 1, 0)
    camera_blocks = obs_camera.reshape(count, SPAN)

    def add_cameras(carry, inputs):
        piece, named = inputs
        onehot = (named[:, None] == camera_of_slot[None, :]).astype(jnp.bfloat16)
        return (carry + exact_dot(piece, onehot.astype(jnp.float32)), None)

    partial_value, unused = lax.scan(
        add_cameras, jnp.zeros((width, cameras), jnp.float32), (term_blocks, camera_blocks)
    )
    split = partial_value.reshape(width, lax.axis_size("pts"), lax.axis_size("grp"), owned_count)
    split = sum_at_owner(split, "grp", 2)
    split = sum_at_owner(split, "pts", 1)
    owned = split.reshape(width, owned_count)
    inverse = chol_inverse(owned, pairs)
    outgoing = jnp.stack([inverse[row_at * 9 + col_at] for row_at, col_at in pairs], 0)
    table = lax.all_gather(outgoing, ("pts", "grp"), axis=1, tiled=True)

    def pick_cameras(carry, named):
        onehot = (named[:, None] == camera_of_slot[None, :]).astype(jnp.bfloat16)
        return (carry, exact_dot(table, onehot.astype(jnp.float32).T))

    unused, picked = lax.scan(pick_cameras, 0, camera_blocks)
    picked = jnp.moveaxis(picked, 0, 1).reshape(width, count * SPAN)
    position = {pair: pos for pos, pair in enumerate(pairs)}
    locate = {}
    for row_at in range(9):
        for col_at in range(9):
            if (row_at, col_at) in position:
                locate[row_at, col_at] = position[row_at, col_at]
            else:
                locate[row_at, col_at] = position[col_at, row_at]
    precond = apply_inverse(picked, reduced, locate)
    return (inverse, precond)


def solution(mesh):
    in_specs = (
        P(None, ("pts", "grp")),
        P(None, ("pts", "grp")),
        P(None, ("pts", "grp")),
        P(("pts", "grp")),
        P(("pts", "grp")),
        P(),
    )
    out_specs = (P(None, ("pts", "grp")), P(None, ("pts", "grp")))
    return jax.shard_map(shards, mesh=mesh, in_specs=in_specs, out_specs=out_specs, check_vma=False)
```

profile of v0, /device:TPU:1, one launch (start us, length us, event | category | flops | bytes accessed | tf_op | source)
XLA Modules:
  0.0 349.4 jit_solution(5146475019787182314)
XLA Ops:
  1.6 1.9 multiply_add_fusion.87
  3.5 2.0 multiply_add_fusion.82
  6.0 70.7 %while.44 = (s32[]{:T(128)}, f32[9,2560]{1,0:T(8,128)S(1)}, s32[16]{0:T(128)S(1)}, f32[16,9,512]{2,1,0:T(8,128)S(1)}, s32[16,512]{1,0:T(8,128)S(1)}, /*index=5*/s32[]{:T(128)}, s32[]{:T(128)}, s32[]{:T(128)}) while((s32[]{:T(128)}, f32[9,2560]{1,0:T(8,128)S(1)}, s32[16]{0:T(128)S(1)}, f32[16,9,512]{2,1,0:T(8,128)S(1)}, ...), condition=%wide.region_1.2_spmd.clone, body=%wide.region_0.1_spmd.clone.sunk | while | flops 28578820 | bytes 127135 | solution.py:54
  77.1 64.2 %while.45 = (s32[]{:T(128)}, f32[16,9,512]{2,1,0:T(8,128)S(1)}, s32[16]{0:T(128)S(1)}, f32[9,2560]{1,0:T(8,128)S(1)}, s32[16,512]{1,0:T(8,128)S(1)}, /*index=5*/s32[]{:T(128)}, s32[]{:T(128)}, s32[]{:T(128)}) while((s32[]{:T(128)}, f32[16,9,512]{2,1,0:T(8,128)S(1)}, s32[16]{0:T(128)S(1)}, f32[9,2560]{1,0:T(8,128)S(1)}, ...), condition=%wide.region_3.4_spmd.clone, body=%wide.region_2.3_spmd.clone.sunk | while | flops 28574212 | bytes 71835 | solution.py:87
  144.5 8.2 %scatter_custom_fusion = s32[2048]{0:T(1024)S(1)} fusion(s32[2048]{0:T(1024)S(1)} %compare_select_fusion, s32[2048]{0:T(1024)S(1)} %iota.10, s32[]{:T(128)} %copy.541), kind=kCustom, calls=%fused_computation.145 | custom fusion | bytes 8196 | tf_op jit(solution)/shard_map/scatter | solution.py:186
  158.0 6.3 %stack.335 = f32[45,16,512]{2,0,1:T(8,128)S(1)} concatenate(f32[1,16,512]{2,0,1:T(1,128)} %bitcast.291, f32[1,16,512]{2,0,1:T(1,128)} %bitcast.290, f32[1,16,512]{2,0,1:T(1,128)} %bitcast.270, f32[1,16,512]{2,0,1:T(1,128)} %bitcast.289, f32[1,16,512]{2,0,1:T(1,128)S(1)} %bitcast.269, f32[1,16,512]{2,0,1:T(1,128)} %bitcast.276, f32[1,16,512]{2,0,1:T(1,128)} %bitcast.288, ...), dimensions={0} | concatenate | bytes 2949120 | tf_op jit(solution)/shard_map/stack | solution.py:124
  164.3 38.5 %while.46 = (s32[]{:T(128)}, f32[45,2048]{1,0:T(8,128)S(1)}, f32[16,45,512]{2,1,0:T(8,128)S(1)}, s32[16,512]{1,0:T(8,128)}, s32[2048]{0:T(1024)S(1)}, /*index=5*/s32[]{:T(128)}, s32[]{:T(128)}) while((s32[]{:T(128)}, f32[45,2048]{1,0:T(8,128)S(1)}, f32[16,45,512]{2,1,0:T(8,128)S(1)}, s32[16,512]{1,0:T(8,128)}, s32[2048]{0:T(1024)S(1)}, ...), condition=%wide.region_6.7_spmd.clone, body=%wide.region_5.6_spmd.clone.sunk | while | flops 567463936 | bytes 874599 | solution.py:197
  169.8 1.7 fusion.91
  172.3 1.7 fusion.91
  204.5 5.0 %all_to_all.10 = f32[2,1,46080]{2,1,0:T(1,128)S(1)} all-to-all(f32[2,1,46080]{2,1,0:T(1,128)S(1)} %reshape.4789), channel_id=1, replica_groups=mesh['pts'=64,'grp'=2] {'grp'}, dimensions={0} | all-to-all | bytes 737280 | tf_op jit(solution)/shard_map/all_to_all | solution.py:19
  210.0 1.8 reduce.4
  214.0 11.3 %all-to-all-start.1 = ((f32[64,1,720]{2,1,0:T(1,128)}), f32[64,1,720]{2,1,0:T(1,128)S(1)}, u32[]{:S(2)}, u32[]{:S(2)}) async-start(f32[64,1,720]{2,1,0:T(1,128)} %reshape.4791), calls=%async_computation.1 | async-start | bytes 393216 | tf_op jit(solution)/shard_map/all_to_all | solution.py:19
  225.5 8.6 %all-to-all-done.1 = f32[64,1,720]{2,1,0:T(1,128)S(1)} async-done(((f32[64,1,720]{2,1,0:T(1,128)}), f32[64,1,720]{2,1,0:T(1,128)S(1)}, u32[]{:S(2)}, u32[]{:S(2)}) %all-to-all-start.1) | async-done | bytes 184352 | tf_op jit(solution)/shard_map/all_to_all | solution.py:19
  245.2 35.8 %all_gather.3 = f32[45,2048]{0,1:T(8,128)S(1)} all-gather(f32[45,16]{0,1:T(8,128)S(1)} %stack.337), channel_id=1, replica_groups=mesh['pts'=64,'grp'=2] {'pts','grp'}, dimensions={1}, use_global_device_ids=true | all-gather | bytes 371520 | tf_op jit(solution)/shard_map/all_gather | solution.py:206
  282.0 61.7 %while.43 = (s32[]{:T(128)}, f32[16,45,512]{2,1,0:T(8,128)S(1)}, s32[16,512]{1,0:T(8,128)}, s32[2048]{0:T(1024)S(1)}, f32[45,2048]{1,0:T(8,128)}, /*index=5*/s32[]{:T(128)}) while((s32[]{:T(128)}, f32[16,45,512]{2,1,0:T(8,128)S(1)}, s32[16,512]{1,0:T(8,128)}, s32[2048]{0:T(1024)S(1)}, f32[45,2048]{1,0:T(8,128)}, /*index=5*/s32[]{:T(128)}) %tuple.423), condition=%wide.region_10.11_spmd, body=%wide.region_9.10_spmd.sunk | while | flops 567279616 | bytes 481365 | solution.py:212
  282.7 3.1 fusion.85
  286.6 3.1 fusion.85
  290.4 3.1 fusion.85
  294.3 3.1 fusion.85
  298.2 3.1 fusion.85
  302.0 3.1 fusion.85
  305.9 3.1 fusion.85
  309.7 3.1 fusion.85
  313.6 3.1 fusion.85
  317.4 3.1 fusion.85
  321.3 3.1 fusion.85
  325.2 3.1 fusion.85
  329.0 3.1 fusion.85
  332.9 3.1 fusion.85
  336.7 3.1 fusion.85
  340.6 3.1 fusion.85
  347.5 1.8 stack.338
  (336 shorter events, 146.2 us)
Async XLA Ops:
  76.7 65.5 %copy-start = (f32[18,8192]{1,0:T(8,128)S(1)}, f32[18,8192]{1,0:T(8,128)}, u32[]{:S(2)}) copy-start(f32[18,8192]{1,0:T(8,128)} %param.14) | copy-start | bytes 1769476
  76.7 65.5 %copy-start.1 = (f32[6,8192]{1,0:T(8,128)S(1)}, f32[6,8192]{1,0:T(8,128)}, u32[]{:S(2)}) copy-start(f32[6,8192]{1,0:T(8,128)} %param.15) | copy-start | bytes 589828
  141.3 2.5 copy-start.7
  141.3 2.5 copy-start.6
  212.3 13.0 %copy-start.2 = (f32[2,8192]{1,0:T(2,128)S(1)}, f32[2,8192]{1,0:T(2,128)}, u32[]{:S(2)}) copy-start(f32[2,8192]{1,0:T(2,128)} %param.16) | copy-start | bytes 196612
  212.3 13.0 %copy-start.3 = (f32[1,16,512]{2,0,1:T(1,128)S(1)}, f32[1,16,512]{2,0,1:T(1,128)}, u32[]{:S(2)}) copy-start(f32[1,16,512]{2,0,1:T(1,128)} %get-tuple-element.485) | copy-start | bytes 98308
  212.3 13.0 %copy-start.4 = (f32[1,16,512]{2,0,1:T(1,128)S(1)}, f32[1,16,512]{2,0,1:T(1,128)}, u32[]{:S(2)}) copy-start(f32[1,16,512]{2,0,1:T(1,128)} %get-tuple-element.486) | copy-start | bytes 98308
  212.4 13.0 %copy-start.5 = (f32[1,16,512]{2,0,1:T(1,128)S(1)}, f32[1,16,512]{2,0,1:T(1,128)}, u32[]{:S(2)}) copy-start(f32[1,16,512]{2,0,1:T(1,128)} %get-tuple-element.487) | copy-start | bytes 98308
  214.0 20.2 %all-to-all-start.1 = ((f32[64,1,720]{2,1,0:T(1,128)}), f32[64,1,720]{2,1,0:T(1,128)S(1)}, u32[]{:S(2)}, u32[]{:S(2)}) async-start(f32[64,1,720]{2,1,0:T(1,128)} %reshape.4791), calls=%async_computation.1 | async-start | bytes 393216 | tf_op jit(solution)/shard_map/all_to_all | solution.py:19
where the time goes:
time: 354 us; the launch traced here: 349 us
  matrix products  93.8 us (26%)
  local copies, waits for them, and re-layouts  87.4 us (25%)
  loops' own time  66.1 us (19%)
  blocking collectives  40.8 us (12%)
  other arithmetic  40.1 us (11%)
  starting transfers between devices  11.3 us (3%)
  waiting for transfers between devices  8.62 us (2%)
    dot_general x64, matrix products, exact_dot(): jnp.dot(left, right, precision=lax.Precision.HIGHEST, preferred_element_t...  93.8 us
    dynamic_slice x64, local copies, waits for them, and re-layouts, point_table(): lax.scan(add_block, jnp.zeros((9, npoints + SPAN), jnp.float32), (pieces,...  44.2 us
    all_gather x1, blocking collectives, shards(): table = lax.all_gather(outgoing, ('pts', 'grp'), axis=1, tiled=True)  35.8 us
    another operation x1, loops' own time, point_table(): lax.scan(add_block, jnp.zeros((9, npoints + SPAN), jnp.float32), (pieces,...  32.9 us
    another operation x1, loops' own time, point_table(): unused, picked = lax.scan(pick_block, 0, (point_rows, firsts))  32.5 us
    all_to_all x1, starting transfers between devices, sum_at_owner(): parts = lax.all_to_all(split_up(value, dim, length), axis, 0, 0, tiled=True)  11.3 us
    sub x16, other arithmetic, add_block(): points[:, None] - first == window_ids[None, :]  10.9 us
    sub x16, other arithmetic, pick_block(): points[:, None] - first == window_ids[None, :]  10.9 us
  transfers between devices with their start and end apart: 1, of which 1 were waited for; matrix products, arithmetic and copies ran while one was open for 0% of the time, Pallas kernels for 0%

commit v1 on v0

--- a/solution.py
+++ b/solution.py
@@ -203,7 +203,10 @@
     owned = split.reshape(width, owned_count)
     inverse = chol_inverse(owned, pairs)
     outgoing = jnp.stack([inverse[row_at * 9 + col_at] for row_at, col_at in pairs], 0)
-    table = lax.all_gather(outgoing, ("pts", "grp"), axis=1, tiled=True)
+    table = jnp.concatenate(
+        lax.all_to_all(jnp.stack([outgoing] * lax.axis_size(("pts", "grp"))), ("pts", "grp"), 0, 0),
+        axis=1,
+    )
 
     def pick_cameras(carry, named):
         onehot = (named[:, None] == camera_of_slot[None, :]).astype(jnp.bfloat16)

time: 354 us -> 334 us (0.944)
  blocking collectives: 40.8 us -> 25 us
  local copies, waits for them, and re-layouts: 87.4 us -> 96.7 us
  starting transfers between devices: 11.3 us -> 5.28 us
  matrix products: 93.8 us -> 88.1 us
  loops' own time: 66.1 us -> 62.3 us
    all_gather x1 -> x0, blocking collectives: 35.8 us -> none  [shards(): table = lax.all_gather(outgoing, ('pts', 'grp'), axis=1, tiled=True)]
    all_to_all x1 -> x2, blocking collectives: 5.03 us -> 25 us  [sum_at_owner(): parts = lax.all_to_all(split_up(value, dim, length), axis, 0, 0, tiled=True)]
    slice x2, local copies, waits for them, and re-layouts: 1.12 us -> 7.2 us  [apply_inverse(): value = value + picked[locate[row_at, col_at]] * reduced[col_at]]
    all_to_all x1, starting transfers between devices: 11.3 us -> 5.28 us  [shards(): lax.all_to_all(jnp.stack([outgoing] * lax.axis_size(('pts', 'grp'))), ('p...]
    dot_general x64, matrix products: 93.8 us -> 88.1 us  [exact_dot(): jnp.dot(left, right, precision=lax.Precision.HIGHEST, preferred_element_t...]
    unnamed x67 -> x70, local copies, waits for them, and re-layouts: 6.46 us -> 8.65 us
where the time goes in v1:
time: 334 us; the launch traced here: 330 us
  local copies, waits for them, and re-layouts  96.7 us (29%)
  matrix products  88.1 us (26%)
  loops' own time  62.3 us (19%)
  other arithmetic  40.4 us (12%)
  blocking collectives  25 us (7%)
  waiting for transfers between devices  11.1 us (3%)
  starting transfers between devices  5.28 us (2%)
    dot_general x64, matrix products, exact_dot(): jnp.dot(left, right, precision=lax.Precision.HIGHEST, preferred_element_t...  88.1 us
    dynamic_slice x64, local copies, waits for them, and re-layouts, point_table(): lax.scan(add_block, jnp.zeros((9, npoints + SPAN), jnp.float32), (pieces,...  44.3 us
    another operation x1, loops' own time, point_table(): lax.scan(add_block, jnp.zeros((9, npoints + SPAN), jnp.float32), (pieces,...  31.1 us
    another operation x1, loops' own time, point_table(): unused, picked = lax.scan(pick_block, 0, (point_rows, firsts))  30.8 us
    all_to_all x2, blocking collectives, sum_at_owner(): parts = lax.all_to_all(split_up(value, dim, length), axis, 0, 0, tiled=True)  25 us
    all_to_all x1, waiting for transfers between devices, shards(): lax.all_to_all(jnp.stack([outgoing] * lax.axis_size(('pts', 'grp'))), ('p...  11.1 us
    sub x16, other arithmetic, add_block(): points[:, None] - first == window_ids[None, :]  10.3 us
    sub x16, other arithmetic, pick_block(): points[:, None] - first == window_ids[None, :]  10.3 us
  transfers between devices with their start and end apart: 1, of which 1 were waited for; matrix products, arithmetic and copies ran while one was open for 0% of the time, Pallas kernels for 0%

profile of v1, /device:TPU:1, one launch (start us, length us, event | category | flops | bytes accessed | tf_op | source)
XLA Modules:
  0.0 330.2 jit_solution(6855142550073697967)
XLA Ops:
  1.6 1.9 multiply_add_fusion.87
  3.5 2.0 multiply_add_fusion.82
  6.0 68.4 %while.44 = (s32[]{:T(128)}, f32[9,2560]{1,0:T(8,128)S(1)}, s32[16]{0:T(128)S(1)}, f32[16,9,512]{2,1,0:T(8,128)S(1)}, s32[16,512]{1,0:T(8,128)S(1)}, /*index=5*/s32[]{:T(128)}, s32[]{:T(128)}, s32[]{:T(128)}) while((s32[]{:T(128)}, f32[9,2560]{1,0:T(8,128)S(1)}, s32[16]{0:T(128)S(1)}, f32[16,9,512]{2,1,0:T(8,128)S(1)}, ...), condition=%wide.region_1.2_spmd.clone, body=%wide.region_0.1_spmd.clone.sunk | while | flops 28578820 | bytes 127135 | solution.py:54
  74.8 62.0 %while.45 = (s32[]{:T(128)}, f32[16,9,512]{2,1,0:T(8,128)S(1)}, s32[16]{0:T(128)S(1)}, f32[9,2560]{1,0:T(8,128)S(1)}, s32[16,512]{1,0:T(8,128)S(1)}, /*index=5*/s32[]{:T(128)}, s32[]{:T(128)}, s32[]{:T(128)}) while((s32[]{:T(128)}, f32[16,9,512]{2,1,0:T(8,128)S(1)}, s32[16]{0:T(128)S(1)}, f32[9,2560]{1,0:T(8,128)S(1)}, ...), condition=%wide.region_3.4_spmd.clone, body=%wide.region_2.3_spmd.clone.sunk | while | flops 28574212 | bytes 71835 | solution.py:87
  139.9 8.2 %scatter_custom_fusion = s32[2048]{0:T(1024)S(1)} fusion(s32[2048]{0:T(1024)S(1)} %compare_select_fusion, s32[2048]{0:T(1024)S(1)} %iota.10, s32[]{:T(128)} %copy.543), kind=kCustom, calls=%fused_computation.145 | custom fusion | bytes 8196 | tf_op jit(solution)/shard_map/scatter | solution.py:186
  153.4 6.3 %stack.178 = f32[45,16,512]{2,0,1:T(8,128)S(1)} concatenate(f32[1,16,512]{2,0,1:T(1,128)} %bitcast.298, f32[1,16,512]{2,0,1:T(1,128)} %bitcast.297, f32[1,16,512]{2,0,1:T(1,128)} %bitcast.277, f32[1,16,512]{2,0,1:T(1,128)} %bitcast.296, f32[1,16,512]{2,0,1:T(1,128)S(1)} %bitcast.276, f32[1,16,512]{2,0,1:T(1,128)} %bitcast.283, f32[1,16,512]{2,0,1:T(1,128)} %bitcast.295, ...), dimensions={0} | concatenate | bytes 2949120 | tf_op jit(solution)/shard_map/stack | solution.py:124
  159.7 38.5 %while.46 = (s32[]{:T(128)}, f32[45,2048]{1,0:T(8,128)S(1)}, f32[16,45,512]{2,1,0:T(8,128)S(1)}, s32[16,512]{1,0:T(8,128)}, s32[2048]{0:T(1024)S(1)}, /*index=5*/s32[]{:T(128)}, s32[]{:T(128)}) while((s32[]{:T(128)}, f32[45,2048]{1,0:T(8,128)S(1)}, f32[16,45,512]{2,1,0:T(8,128)S(1)}, s32[16,512]{1,0:T(8,128)}, s32[2048]{0:T(1024)S(1)}, ...), condition=%wide.region_6.7_spmd.clone, body=%wide.region_5.6_spmd.clone.sunk | while | flops 567463936 | bytes 874599 | solution.py:197
  199.9 5.0 %all_to_all.15 = f32[2,1,46080]{2,1,0:T(1,128)S(1)} all-to-all(f32[2,1,46080]{2,1,0:T(1,128)S(1)} %reshape.4799), channel_id=1, replica_groups=mesh['pts'=64,'grp'=2] {'grp'}, dimensions={0} | all-to-all | bytes 737280 | tf_op jit(solution)/shard_map/all_to_all | solution.py:19
  208.7 20.0 %all_to_all.16 = f32[64,1,720]{2,1,0:T(1,128)S(1)} all-to-all(f32[64,1,720]{2,1,0:T(1,128)S(1)} %reshape.4801), channel_id=1, replica_groups=mesh['pts'=64,'grp'=2] {'pts'}, dimensions={0} | all-to-all | bytes 368640 | tf_op jit(solution)/shard_map/all_to_all | solution.py:19
  238.9 2.1 reshape.4803
  241.0 5.3 %all-to-all-start.2 = ((f32[128,1,720]{2,1,0:T(1,128)}), f32[128,1,720]{2,1,0:T(1,128)S(1)}, u32[]{:S(2)}, u32[]{:S(2)}) async-start(f32[128,1,720]{2,1,0:T(1,128)} %reshape.4803), calls=%async_computation.2 | async-start | bytes 786432 | tf_op jit(solution)/shard_map/all_to_all | solution.py:207
  247.4 11.1 %all-to-all-done.2 = f32[128,1,720]{2,1,0:T(1,128)S(1)} async-done(((f32[128,1,720]{2,1,0:T(1,128)}), f32[128,1,720]{2,1,0:T(1,128)S(1)}, u32[]{:S(2)}, u32[]{:S(2)}) %all-to-all-start.2) | async-done | bytes 368672 | tf_op jit(solution)/shard_map/all_to_all | solution.py:207
  261.1 55.7 %while.43 = (s32[]{:T(128)}, f32[16,45,512]{2,1,0:T(8,128)}, s32[16,512]{1,0:T(8,128)}, s32[2048]{0:T(1024)S(1)}, f32[45,2048]{1,0:T(8,128)S(1)}, /*index=5*/s32[]{:T(128)}) while((s32[]{:T(128)}, f32[16,45,512]{2,1,0:T(8,128)}, s32[16,512]{1,0:T(8,128)}, s32[2048]{0:T(1024)S(1)}, f32[45,2048]{1,0:T(8,128)S(1)}, /*index=5*/s32[]{:T(128)}) %tuple.423), condition=%wide.region_10.11_spmd, body=%wide.region_9.10_spmd.sunk | while | flops 567279616 | bytes 481365 | solution.py:215
  261.9 2.8 fusion.85
  265.4 2.8 fusion.85
  268.8 2.7 fusion.85
  272.3 2.7 fusion.85
  275.8 2.8 fusion.85
  279.3 2.8 fusion.85
  282.8 2.8 fusion.85
  286.2 2.8 fusion.85
  289.7 2.8 fusion.85
  293.2 2.8 fusion.85
  296.7 2.8 fusion.85
  300.2 2.8 fusion.85
  303.6 2.8 fusion.85
  307.1 2.7 fusion.85
  310.6 2.8 fusion.85
  314.1 2.8 fusion.85
  316.8 1.8 fusion.68
  318.6 3.6 %fusion.67 = (f32[1,16,512]{2,0,1:T(1,128)S(1)}, f32[1,16,512]{2,0,1:T(1,128)S(1)}, f32[1,16,512]{2,0,1:T(1,128)S(1)}, f32[1,16,512]{2,0,1:T(1,128)S(1)}, f32[1,...) fusion(f32[45,16,512]{2,0,1:T(8,128)} %bitcast.185), kind=kLoop, calls=%fused_computation.289 | loop fusion | bytes 1245184 | tf_op jit(solution)/shard_map/slice | solution.py:172
  322.2 3.6 %fusion.66 = (f32[1,16,512]{2,0,1:T(1,128)S(1)}, f32[1,16,512]{2,0,1:T(1,128)S(1)}, f32[1,16,512]{2,0,1:T(1,128)S(1)}, f32[1,16,512]{2,0,1:T(1,128)S(1)}, f32[1,...) fusion(f32[45,16,512]{2,0,1:T(8,128)} %bitcast.186), kind=kLoop, calls=%fused_computation.288 | loop fusion | bytes 1245184 | tf_op jit(solution)/shard_map/slice | solution.py:172
  (340 shorter events, 151.6 us)
Async XLA Ops:
  74.4 63.3 %copy-start = (f32[18,8192]{1,0:T(8,128)S(1)}, f32[18,8192]{1,0:T(8,128)}, u32[]{:S(2)}) copy-start(f32[18,8192]{1,0:T(8,128)} %param.14) | copy-start | bytes 1769476
  74.4 63.2 %copy-start.1 = (f32[6,8192]{1,0:T(8,128)S(1)}, f32[6,8192]{1,0:T(8,128)}, u32[]{:S(2)}) copy-start(f32[6,8192]{1,0:T(8,128)} %param.15) | copy-start | bytes 589828
  136.8 2.5 copy-start.7
  136.8 2.5 copy-start.6
  238.8 7.5 %copy-start.2 = (f32[2,8192]{1,0:T(2,128)S(1)}, f32[2,8192]{1,0:T(2,128)}, u32[]{:S(2)}) copy-start(f32[2,8192]{1,0:T(2,128)} %param.16) | copy-start | bytes 196612
  238.8 7.5 %copy-start.3 = (f32[1,16,512]{2,0,1:T(1,128)S(1)}, f32[1,16,512]{2,0,1:T(1,128)}, u32[]{:S(2)}) copy-start(f32[1,16,512]{2,0,1:T(1,128)} %get-tuple-element.485) | copy-start | bytes 98308
  238.8 7.5 %copy-start.4 = (f32[1,16,512]{2,0,1:T(1,128)S(1)}, f32[1,16,512]{2,0,1:T(1,128)}, u32[]{:S(2)}) copy-start(f32[1,16,512]{2,0,1:T(1,128)} %get-tuple-element.486) | copy-start | bytes 98308
  238.8 7.5 %copy-start.5 = (f32[1,16,512]{2,0,1:T(1,128)S(1)}, f32[1,16,512]{2,0,1:T(1,128)}, u32[]{:S(2)}) copy-start(f32[1,16,512]{2,0,1:T(1,128)} %get-tuple-element.487) | copy-start | bytes 98308
  241.0 17.5 %all-to-all-start.2 = ((f32[128,1,720]{2,1,0:T(1,128)}), f32[128,1,720]{2,1,0:T(1,128)S(1)}, u32[]{:S(2)}, u32[]{:S(2)}) async-start(f32[128,1,720]{2,1,0:T(1,128)} %reshape.4803), calls=%async_computation.2 | async-start | bytes 786432 | tf_op jit(solution)/shard_map/all_to_all | solution.py:207
